TPU v7x, 32 devices: a whole 2x2x4 slice. The times are simulated.
32 devices in a mesh: dp: 4 (over x, core), section: 2 (over y), expert: 4 (over z).
Axes of the slice: x: 2, y: 2, z: 4, core: 2. Of those that a mesh axis runs over, the one named last changes fastest.
Arguments:
- paths_in: bfloat16 [2, 256, 4, 7168], P(None, 'expert', None, 'dp'), may hold values from -12 to 12
- path_proj: bfloat16 [2, 24, 4, 7168], P('section', None, None, 'dp'), may hold values from -0.03125 to 0.03125
- coef_bias: float32 [2, 24], P('section'), may hold values from -4 to 4
- norm_gain: bfloat16 [2, 7168], P('section', 'dp'), may hold values from 0.25 to 1.75
- w_gate_up: bfloat16 [2, 4, 7168, 2, 512], P('section', 'expert', 'dp'), may hold values from -0.0625 to 0.0625
- w_down: bfloat16 [2, 4, 512, 7168], P('section', 'expert', None, 'dp'), may hold values from -0.1875 to 0.1875
- routes: int32 [2, 2, 256, 1], P('section', None, 'expert'), may hold values from 0 to 1; in each aligned block of 64 rows (0 to 63, 64 to 127, ..., all dimensions but the last counted through in order) at most 32 rows name the same one
- route_gate: float32 [2, 2, 256, 1], P('section', None, 'expert'), may hold values from 0.2 to 1
Outputs:
- paths_out: bfloat16 [2, 2, 256, 4, 7168], P('section', None, 'expert', None, 'dp')
Inputs may be any that keep to these rules, and one draw needn't show every extreme that they name: `routes`: each row names exactly one expert. In each aligned block of 64 rows (the tokens of one index of expert in one layer and micro-batch) no expert is named more than 32 times, a bound that some block reaches.
All inputs are finite; a program needn't handle non-finite values.
Results may differ from a plain program's by a relative error of at most 0.014.
Values may be sent and summed in bfloat16 or wider, within the bound.
A program may use at most 64 MiB of HBM per device.

v0:
```python
import jax
import jax.numpy as jnp
from jax import lax
from jax.sharding import PartitionSpec as P

D = 7168
RESIDUAL_STREAMS = 4
SINK = 20
EPSILON = 1e-06


def passed_along(value, axis, steps):
    count = lax.axis_size(axis)
    leading, last = (max(0, -steps), min(count, count - steps))
    return lax.ppermute(value, axis, [(source, source + steps) for source in range(leading, last)])


def doubly_stochastic_project(stream_mixer):
    for repeat in range(SINK):
        stream_mixer = stream_mixer / jnp.sum(stream_mixer, axis=2, keepdims=True)
        stream_mixer = stream_mixer / jnp.sum(stream_mixer, axis=1, keepdims=True)
    return stream_mixer


def expert_block(received, gate_up, down_proj):
    sources, items, width = received.shape
    slot_rows = received.reshape(sources * items, width)
    inner = down_proj.shape[0]
    hidden_pre = jnp.dot(slot_rows, gate_up, preferred_element_type=jnp.float32)
    summed = lax.psum(hidden_pre, "dp")
    hidden = (jax.nn.silu(summed[:, :inner]) * summed[:, inner:]).astype(jnp.bfloat16)
    expert_output_rows = jnp.dot(hidden, down_proj, preferred_element_type=jnp.float32)
    expert_output_rows = expert_output_rows.astype(jnp.bfloat16).reshape(sources, items, width)
    return lax.all_to_all(expert_output_rows, "expert", split_axis=0, concat_axis=0, tiled=True)


def mix_layer(residual, path_proj, coef_bias, norm_gain, gate_up, down_proj, routes_now, gates_now):
    rows, paths, width = residual.shape
    widened = residual.astype(jnp.float32)
    square_part = jnp.sum(widened * widened, axis=(1, 2))
    projected = jnp.einsum("tsd,csd->tc", residual, path_proj, preferred_element_type=jnp.float32)
    path_gram = jnp.einsum("tid,tjd->tij", residual, residual, preferred_element_type=jnp.float32)
    square_sum, projected, path_gram = lax.psum((square_part, projected, path_gram), "dp")
    router_scores = (
        projected * lax.rsqrt(square_sum / (RESIDUAL_STREAMS * D) + EPSILON)[:, None]
        + coef_bias[None, :]
    )
    pre_weight = jax.nn.sigmoid(router_scores[:, :RESIDUAL_STREAMS])
    post_weight = 2.0 * jax.nn.sigmoid(router_scores[:, RESIDUAL_STREAMS : 2 * RESIDUAL_STREAMS])
    stream_mixer = doubly_stochastic_project(
        jnp.exp(router_scores[:, 2 * RESIDUAL_STREAMS :]).reshape(
            -1, RESIDUAL_STREAMS, RESIDUAL_STREAMS
        )
    )
    merged = jnp.sum(pre_weight[:, :, None] * widened, axis=1)
    width_sum = jnp.einsum(
        "ti,tij,tj->t", pre_weight, path_gram, pre_weight, precision=lax.Precision.HIGHEST
    )
    normed = (
        merged
        * lax.rsqrt(width_sum / D + EPSILON)[:, None]
        * norm_gain.astype(jnp.float32)[None, :]
    ).astype(jnp.bfloat16)
    expert_count = lax.axis_size("expert") // 2
    selected_expert_count = routes_now.shape[1]
    capacity = min(rows, max(2, (rows * selected_expert_count + expert_count - 1) // expert_count))
    slot_count = expert_count * capacity
    flat_routes = routes_now.reshape(-1)
    chosen = (flat_routes[:, None] == jnp.arange(expert_count, dtype=jnp.int32)[None, :]).astype(
        jnp.int32
    )
    earlier = jnp.cumsum(chosen, axis=0) - chosen
    rank_within = jnp.sum(earlier * chosen, axis=1)
    slot_of = flat_routes * capacity + rank_within
    slot_match = jnp.arange(slot_count, dtype=jnp.int32)[:, None] == slot_of[None, :]
    dispatch_map = jnp.sum(
        slot_match.reshape(slot_count, rows, selected_expert_count).astype(jnp.int32), axis=2
    ).astype(jnp.bfloat16)
    gate_spread = jnp.where(slot_match, gates_now.reshape(-1)[None, :], 0.0)
    combine_map = jnp.sum(gate_spread.reshape(slot_count, rows, selected_expert_count), axis=2).T
    outgoing = jnp.dot(dispatch_map, normed, preferred_element_type=jnp.float32).astype(
        jnp.bfloat16
    )
    outgoing = outgoing.reshape(expert_count, 1, capacity, width)
    outgoing = jnp.broadcast_to(outgoing, (expert_count, 2, capacity, width)).reshape(
        2 * expert_count, capacity, width
    )
    returned = expert_block(
        lax.all_to_all(outgoing, "expert", split_axis=0, concat_axis=0, tiled=True),
        gate_up=gate_up,
        down_proj=down_proj,
    )
    halves = returned.reshape(expert_count, 2, capacity, width).astype(jnp.float32)
    expert_weighted_total = halves[:, 0] + halves[:, 1]
    branch = jnp.dot(
        combine_map,
        expert_weighted_total.reshape(slot_count, width),
        precision=lax.Precision.HIGHEST,
    )
    carried = jnp.einsum("tji,tid->tjd", stream_mixer, widened, precision=lax.Precision.HIGHEST)
    return (carried + post_weight[:, :, None] * branch[:, None, :]).astype(jnp.bfloat16)


def body(paths_in, path_proj, coef_bias, norm_gain, w_gate_up, w_down, routes, route_gate):
    section_index = lax.axis_index("section")
    section_count = lax.axis_size("section")
    micro_count = paths_in.shape[0]
    gate_up = w_gate_up[0, 0].reshape(w_gate_up.shape[2], -1)
    down_proj = w_down[0, 0]
    incoming = jnp.zeros(paths_in.shape[1:], jnp.bfloat16)
    results = jnp.zeros(paths_in.shape, jnp.bfloat16)
    slot_index = jnp.arange(micro_count, dtype=jnp.int32)
    total_steps = micro_count + section_count - 1
    for time_step in range(total_steps):
        micro_index = time_step - section_index
        clipped = jnp.clip(micro_index, 0, micro_count - 1)
        entering = lax.dynamic_index_in_dim(paths_in, clipped, 0, keepdims=False)
        current = jnp.where(section_index == 0, entering, incoming)
        routes_now = lax.dynamic_index_in_dim(routes[0], clipped, 0, keepdims=False)
        gates_now = lax.dynamic_index_in_dim(route_gate[0], clipped, 0, keepdims=False)
        leaving = mix_layer(
            current,
            path_proj[0],
            coef_bias[0],
            norm_gain[0],
            gate_up,
            down_proj,
            routes_now,
            gates_now,
        )
        results = jnp.where(
            (slot_index == micro_index)[:, None, None, None], leaving[None], results
        )
        if time_step + 1 < total_steps:
            incoming = passed_along(leaving, "section", 1)
    return results[None]


def solution(mesh):
    in_specs = (
        P(None, "expert", None, "dp"),
        P("section", None, None, "dp"),
        P("section", None),
        P("section", "dp"),
        P("section", "expert", "dp", None, None),
        P("section", "expert", None, "dp"),
        P("section", None, "expert", None),
        P("section", None, "expert", None),
    )
    out_specs = P("section", None, "expert", None, "dp")
    return jax.shard_map(body, mesh=mesh, in_specs=in_specs, out_specs=out_specs, check_vma=False)
```

profile of v0, /device:TPU:0, one launch (start us, length us, event | category | flops | bytes accessed | tf_op | source)
XLA Modules:
  0.0 375.9 jit_solution(183301139221659460)
XLA Ops:
  6.5 1.6 constant_dynamic-slice_fusion.6
  8.6 1.2 fusion.129
  10.1 15.1 %all-reduce.2 = (f32[64,24]{0,1:T(8,128)S(1)}, f32[64]{0:T(128)S(1)}, f32[64,4,4]{2,1,0:T(4,128)}) all-reduce(f32[64,24]{0,1:T(8,128)S(1)} %convolution_bitcast_fusion.2, f32[64]{0:T(128)S(1)} %get-tuple-element.18, f32[64,4,4]{2,1,0:T(4,128)S(1)} %fusion.129), channel_id=1, replica_groups=mesh['dp'=4,'section'=2,'expert'=4] {'dp'}, use_global_device_ids=true, to_apply=%region_0.1 | all-reduce | flops 2624 | bytes 20992 | tf_op jit(solution)/shard_map/psum | solution.py:43
  27.2 1.0 fusion.61
  28.2 1.4 copy.290
  29.6 1.5 fusion.265
  31.1 0.9 multiply_reduce_fusion.2
  32.5 1.3 fusion.203
  35.0 1.4 reduce_window_sum.20
  36.4 0.9 select_reduce_fusion.2
  38.8 0.9 convolution_convert_fusion.5
  40.5 4.9 %all-to-all-start = ((bf16[4,32,1792]{2,1,0:T(8,128)(2,1)}), bf16[4,32,1792]{2,1,0:T(8,128)(2,1)S(1)}, u32[]{:S(2)}, u32[]{:S(2)}) async-start(bf16[4,32,1792]{2,1,0:T(8,128)(2,1)} %bitcast.125), calls=%async_computation | async-start | bytes 917504 | tf_op jit(solution)/shard_map/all_to_all | solution.py:89
  45.4 1.3 slice_exponential_fusion.2
  46.7 1.3 reduce_sum.1186
  56.0 0.8 divide_reduce_fusion.50
  58.4 4.8 %copy.306 = bf16[224,8,2,512]{3,1,2,0:T(8,128)(2,1)} copy(bf16[224,8,2,512]{3,2,1,0:T(2,128)(2,1)} %bitcast.121) | data formatting | bytes 7340032
  63.3 1.2 divide_reduce_fusion.45
  64.5 3.5 fusion.266
  68.0 0.8 divide_reduce_fusion.44
  68.9 2.0 divide_reduce_fusion.43
  70.8 31.3 %all-reduce.7.cloned.1.call-done = f32[128,1024]{1,0:T(8,128)} async-done(((f32[128,1024]{1,0:T(8,128)}), f32[128,1024]{1,0:T(8,128)}) %all-reduce.7.cloned.1.call-update) | async-done | bytes 524304 | tf_op jit(solution)/shard_map/psum | solution.py:30
  102.2 2.2 convolution_convert_fusion.2
  104.4 4.6 %all-to-all-start.1 = ((bf16[4,32,1792]{2,1,0:T(8,128)(2,1)}), bf16[4,32,1792]{2,1,0:T(8,128)(2,1)S(1)}, u32[]{:S(2)}, u32[]{:S(2)}) async-start(bf16[4,32,1792]{2,1,0:T(8,128)(2,1)} %bitcast.139), calls=%async_computation.1 | async-start | bytes 917504 | tf_op jit(solution)/shard_map/all_to_all | solution.py:34
  110.6 1.3 multiply_divide_fusion.5
  111.9 1.4 copy.275
  113.4 1.4 copy.277
  114.7 1.3 fusion.199
  116.1 5.1 %all-to-all-done.1 = bf16[4,32,1792]{2,1,0:T(8,128)(2,1)S(1)} async-done(((bf16[4,32,1792]{2,1,0:T(8,128)(2,1)}), bf16[4,32,1792]{2,1,0:T(8,128)(2,1)S(1)}, u32[]{:S(2)}, u32[]{:S(2)}) %all-to-all-start.1) | async-done | bytes 458784 | tf_op jit(solution)/shard_map/all_to_all | solution.py:34
  122.4 3.2 fusion.57
  125.6 4.3 %collective-permute-start = (bf16[64,4,1792]{2,1,0:T(4,128)(2,1)}, bf16[64,4,1792]{2,1,0:T(4,128)(2,1)}, u32[]{:S(2)}, u32[]{:S(2)}) collective-permute-start(bf16[64,4,1792]{2,1,0:T(4,128)(2,1)} %fusion.57), channel_id=1, source_target_pairs={{0,4},{1,5},{2,6},{3,7},{8,12},{9,13},{10,14},{11,15},{16,20},{17,... | collective-permute-start | bytes 2752520 | tf_op jit(solution)/shard_map/ppermute | solution.py:15
  130.9 17.1 %collective-permute-done = bf16[64,4,1792]{2,1,0:T(4,128)(2,1)} collective-permute-done((bf16[64,4,1792]{2,1,0:T(4,128)(2,1)}, bf16[64,4,1792]{2,1,0:T(4,128)(2,1)}, u32[]{:S(2)}, u32[]{:S(2)}) %collective-permute-start) | collective-permute-done | bytes 917536 | tf_op jit(solution)/shard_map/ppermute | solution.py:15
  148.0 2.6 fusion.62
  150.6 1.1 fusion.267
  152.1 11.8 %all-reduce.1 = (f32[64,24]{0,1:T(8,128)S(1)}, f32[64]{0:T(128)S(1)}, f32[64,4,4]{2,1,0:T(4,128)S(1)}) all-reduce(f32[64,24]{0,1:T(8,128)S(1)} %convolution_bitcast_fusion.1, f32[64]{0:T(128)S(1)} %get-tuple-element.16, f32[64,4,4]{2,1,0:T(4,128)S(1)} %fusion.267), channel_id=1, replica_groups=mesh['dp'=4,'section'=2,'expert'=4] {'dp'}, use_global_device_ids=true, to_apply=%region_48.49 | all-reduce | flops 2624 | bytes 20992 | tf_op jit(solution)/shard_map/psum | solution.py:43
  165.4 1.3 fusion.63
  168.5 3.5 all-to-all-start.2
  172.0 1.3 reduce_sum.1229
  184.6 1.2 divide_reduce_fusion.27
  185.8 3.5 fusion.269
  189.3 0.8 divide_reduce_fusion.26
  190.1 2.0 divide_reduce_fusion.25
  192.1 33.4 %all-reduce.9.cloned.1.call-done = f32[128,1024]{1,0:T(8,128)} async-done(((f32[128,1024]{1,0:T(8,128)}), f32[128,1024]{1,0:T(8,128)}) %all-reduce.9.cloned.1.call-update) | async-done | bytes 524304 | tf_op jit(solution)/shard_map/psum | solution.py:30
  225.6 2.2 convolution_convert_fusion.1
  227.8 4.6 %all-to-all-start.3 = ((bf16[4,32,1792]{2,1,0:T(8,128)(2,1)}), bf16[4,32,1792]{2,1,0:T(8,128)(2,1)S(1)}, u32[]{:S(2)}, u32[]{:S(2)}) async-start(bf16[4,32,1792]{2,1,0:T(8,128)(2,1)} %bitcast.137), calls=%async_computation.3 | async-start | bytes 917504 | tf_op jit(solution)/shard_map/all_to_all | solution.py:34
  234.8 1.3 multiply_divide_fusion.4
  236.1 1.5 copy.282
  237.6 1.4 copy.283
  239.0 5.6 %all-to-all-done.3 = bf16[4,32,1792]{2,1,0:T(8,128)(2,1)S(1)} async-done(((bf16[4,32,1792]{2,1,0:T(8,128)(2,1)}), bf16[4,32,1792]{2,1,0:T(8,128)(2,1)S(1)}, u32[]{:S(2)}, u32[]{:S(2)}) %all-to-all-start.3) | async-done | bytes 458784 | tf_op jit(solution)/shard_map/all_to_all | solution.py:34
  245.8 3.0 fusion.58
  248.8 4.3 %collective-permute-start.1 = (bf16[64,4,1792]{2,1,0:T(4,128)(2,1)}, bf16[64,4,1792]{2,1,0:T(4,128)(2,1)}, u32[]{:S(2)}, u32[]{:S(2)}) collective-permute-start(bf16[64,4,1792]{2,1,0:T(4,128)(2,1)} %fusion.58), channel_id=1, source_target_pairs={{0,4},{1,5},{2,6},{3,7},{8,12},{9,13},{10,14},{11,15},{16,20},{17,... | collective-permute-start | bytes 2752520 | tf_op jit(solution)/shard_map/ppermute | solution.py:15
  255.0 16.2 %collective-permute-done.1 = bf16[64,4,1792]{2,1,0:T(4,128)(2,1)} collective-permute-done((bf16[64,4,1792]{2,1,0:T(4,128)(2,1)}, bf16[64,4,1792]{2,1,0:T(4,128)(2,1)}, u32[]{:S(2)}, u32[]{:S(2)}) %collective-permute-start.1) | collective-permute-done | bytes 917536 | tf_op jit(solution)/shard_map/ppermute | solution.py:15
  271.2 2.6 fusion.64
  273.8 1.1 fusion.270
  275.3 11.8 %all-reduce = (f32[64,24]{0,1:T(8,128)S(1)}, f32[64]{0:T(128)S(1)}, f32[64,4,4]{2,1,0:T(4,128)S(1)}) all-reduce(f32[64,24]{0,1:T(8,128)S(1)} %convolution_bitcast_fusion, f32[64]{0:T(128)S(1)} %get-tuple-element.14, f32[64,4,4]{2,1,0:T(4,128)S(1)} %fusion.270), channel_id=1, replica_groups=mesh['dp'=4,'section'=2,'expert'=4] {'dp'}, use_global_device_ids=true, to_apply=%region_96.97 | all-reduce | flops 2624 | bytes 20992 | tf_op jit(solution)/shard_map/psum | solution.py:43
  287.4 1.3 fusion.65
  290.6 3.5 all-to-all-start.4
  294.7 13.0 %all-to-all-done.4 = bf16[4,32,1792]{2,1,0:T(8,128)(2,1)S(1)} async-done(((bf16[4,32,1792]{2,1,0:T(8,128)(2,1)}), bf16[4,32,1792]{2,1,0:T(8,128)(2,1)S(1)}, u32[]{:S(2)}, u32[]{:S(2)}) %all-to-all-start.4) | async-done | bytes 458784 | tf_op jit(solution)/shard_map/all_to_all | solution.py:89
  307.6 3.5 fusion.272
  311.2 32.9 %all-reduce.11.cloned.1.call-done = f32[128,1024]{1,0:T(8,128)} async-done(((f32[128,1024]{1,0:T(8,128)}), f32[128,1024]{1,0:T(8,128)}) %all-reduce.11.cloned.1.call-update) | async-done | bytes 524304 | tf_op jit(solution)/shard_map/psum | solution.py:30
  344.1 2.2 convolution_convert_fusion
  346.4 4.6 %all-to-all-start.5 = ((bf16[4,32,1792]{2,1,0:T(8,128)(2,1)}), bf16[4,32,1792]{2,1,0:T(8,128)(2,1)S(1)}, u32[]{:S(2)}, u32[]{:S(2)}) async-start(bf16[4,32,1792]{2,1,0:T(8,128)(2,1)} %bitcast.138), calls=%async_computation.5 | async-start | bytes 917504 | tf_op jit(solution)/shard_map/all_to_all | solution.py:34
  351.3 11.8 %all-to-all-done.5 = bf16[4,32,1792]{2,1,0:T(8,128)(2,1)S(1)} async-done(((bf16[4,32,1792]{2,1,0:T(8,128)(2,1)}), bf16[4,32,1792]{2,1,0:T(8,128)(2,1)S(1)}, u32[]{:S(2)}, u32[]{:S(2)}) %all-to-all-start.5) | async-done | bytes 458784 | tf_op jit(solution)/shard_map/all_to_all | solution.py:34
  363.9 2.0 fusion.59
  365.9 3.4 select_select_fusion
  (188 shorter events, 44.8 us)
Async XLA Ops:
  6.5 95.6 %copy-start = (bf16[1,1,512,1792]{3,2,1,0:T(8,128)(2,1)S(1)}, bf16[1,1,512,1792]{3,2,1,0:T(8,128)(2,1)}, u32[]{:S(2)}) copy-start(bf16[1,1,512,1792]{3,2,1,0:T(8,128)(2,1)} %param.13) | copy-start | bytes 5505028
  8.5 1.2 copy-start.1
  8.5 16.7 %copy-start.18 = (f32[1,24]{1,0:T(1,128)S(1)}, f32[1,24]{1,0:T(1,128)}, u32[]{:S(2)}) copy-start(f32[1,24]{1,0:T(1,128)} %param.10) | copy-start | bytes 292
  25.4 0.6 copy-start.10
  26.0 0.6 copy-start.11
  33.8 0.5 copy-start.17
  38.0 1.7 copy-start.28
  38.8 1.0 copy-start.2
  40.5 24.0 %all-to-all-start = ((bf16[4,32,1792]{2,1,0:T(8,128)(2,1)}), bf16[4,32,1792]{2,1,0:T(8,128)(2,1)S(1)}, u32[]{:S(2)}, u32[]{:S(2)}) async-start(bf16[4,32,1792]{2,1,0:T(8,128)(2,1)} %bitcast.125), calls=%async_computation | async-start | bytes 917504 | tf_op jit(solution)/shard_map/all_to_all | solution.py:89
  45.4 56.8 %all-reduce.7.cloned.1.call-start = ((), (), s32[]{:S(2)}) async-start(), calls=%async_computation.6 | async-start | bytes 1048576 | tf_op jit(solution)/shard_map/psum | solution.py:30
  58.4 4.9 %copy-start.6 = (f32[64,16]{0,1:T(8,128)S(1)}, f32[64,16]{0,1:T(8,128)}, u32[]{:S(2)}) copy-start(f32[64,16]{0,1:T(8,128)} %slice_exponential_fusion.2) | copy-start | bytes 12292
  104.4 16.7 %all-to-all-start.1 = ((bf16[4,32,1792]{2,1,0:T(8,128)(2,1)}), bf16[4,32,1792]{2,1,0:T(8,128)(2,1)S(1)}, u32[]{:S(2)}, u32[]{:S(2)}) async-start(bf16[4,32,1792]{2,1,0:T(8,128)(2,1)} %bitcast.139), calls=%async_computation.1 | async-start | bytes 917504 | tf_op jit(solution)/shard_map/all_to_all | solution.py:34
  121.1 0.7 copy-start.23
  121.2 0.7 copy-start.29
  121.2 1.2 copy-start.7
  121.2 1.2 copy-start.12
  122.4 7.5 %copy-start.14 = (s32[64]{0:T(128)S(1)}, s32[64]{0:T(128)}, u32[]{:S(2)}) copy-start(s32[64]{0:T(128)} %get-tuple-element.29) | copy-start | bytes 772
  122.4 7.5 %copy-start.16 = (s32[64]{0:T(128)S(1)}, s32[64]{0:T(128)}, u32[]{:S(2)}) copy-start(s32[64]{0:T(128)} %get-tuple-element.31) | copy-start | bytes 772
  125.6 22.4 %collective-permute-start = (bf16[64,4,1792]{2,1,0:T(4,128)(2,1)}, bf16[64,4,1792]{2,1,0:T(4,128)(2,1)}, u32[]{:S(2)}, u32[]{:S(2)}) collective-permute-start(bf16[64,4,1792]{2,1,0:T(4,128)(2,1)} %fusion.57), channel_id=1, source_target_pairs={{0,4},{1,5},{2,6},{3,7},{8,12},{9,13},{10,14},{11,15},{16,20},{17,... | collective-permute-start | bytes 2752520 | tf_op jit(solution)/shard_map/ppermute | solution.py:15
  130.9 36.5 %copy-start.26 = (s32[64]{0:T(128)}, s32[64]{0:T(128)S(1)}, u32[]{:S(2)}) copy-start(s32[64]{0:T(128)S(1)} %multiply_add_fusion.4) | copy-start | bytes 772
  150.6 13.2 %copy-start.19 = (f32[1,24]{1,0:T(1,128)S(1)}, f32[1,24]{1,0:T(1,128)}, u32[]{:S(2)}) copy-start(f32[1,24]{1,0:T(1,128)} %param.10) | copy-start | bytes 292
  151.7 15.7 %copy-start.3 = (f32[1792]{0:T(1024)S(1)}, f32[1792]{0:T(1024)}, u32[]{:S(2)}) copy-start(f32[1792]{0:T(1024)} %copy-done.2) | copy-start | bytes 21508
  168.5 17.3 %all-to-all-start.2 = ((bf16[4,32,1792]{2,1,0:T(8,128)(2,1)}), bf16[4,32,1792]{2,1,0:T(8,128)(2,1)S(1)}, u32[]{:S(2)}, u32[]{:S(2)}) async-start(bf16[4,32,1792]{2,1,0:T(8,128)(2,1)} %bitcast.127), calls=%async_computation.2 | async-start | bytes 917504 | tf_op jit(solution)/shard_map/all_to_all | solution.py:89
  172.0 53.6 %all-reduce.9.cloned.1.call-start = ((), (), s32[]{:S(2)}) async-start(), calls=%async_computation.7 | async-start | bytes 1048576 | tf_op jit(solution)/shard_map/psum | solution.py:30
  173.3 11.3 %copy-start.5 = (f32[64,16]{0,1:T(8,128)S(1)}, f32[64,16]{0,1:T(8,128)}, u32[]{:S(2)}) copy-start(f32[64,16]{0,1:T(8,128)} %slice_exponential_fusion.1) | copy-start | bytes 12292
  227.8 16.7 %all-to-all-start.3 = ((bf16[4,32,1792]{2,1,0:T(8,128)(2,1)}), bf16[4,32,1792]{2,1,0:T(8,128)(2,1)S(1)}, u32[]{:S(2)}, u32[]{:S(2)}) async-start(bf16[4,32,1792]{2,1,0:T(8,128)(2,1)} %bitcast.137), calls=%async_computation.3 | async-start | bytes 917504 | tf_op jit(solution)/shard_map/all_to_all | solution.py:34
  244.5 0.7 copy-start.22
  244.5 0.7 copy-start.27
  244.5 1.2 copy-start.8
  244.5 1.3 copy-start.13
  245.8 7.3 %copy-start.9 = (s32[64,2]{1,0:T(8,128)S(1)}, s32[64,2]{1,0:T(8,128)}, u32[]{:S(2)}) copy-start(s32[64,2]{1,0:T(8,128)} %get-tuple-element.146) | copy-start | bytes 1540
  245.8 9.0 %copy-start.15 = (s32[64]{0:T(128)S(1)}, s32[64]{0:T(128)}, u32[]{:S(2)}) copy-start(s32[64]{0:T(128)} %get-tuple-element.29) | copy-start | bytes 772
  248.8 22.4 %collective-permute-start.1 = (bf16[64,4,1792]{2,1,0:T(4,128)(2,1)}, bf16[64,4,1792]{2,1,0:T(4,128)(2,1)}, u32[]{:S(2)}, u32[]{:S(2)}) collective-permute-start(bf16[64,4,1792]{2,1,0:T(4,128)(2,1)} %fusion.58), channel_id=1, source_target_pairs={{0,4},{1,5},{2,6},{3,7},{8,12},{9,13},{10,14},{11,15},{16,20},{17,... | collective-permute-start | bytes 2752520 | tf_op jit(solution)/shard_map/ppermute | solution.py:15
  255.0 34.4 %copy-start.24 = (s32[64]{0:T(128)}, s32[64]{0:T(128)S(1)}, u32[]{:S(2)}) copy-start(s32[64]{0:T(128)S(1)} %multiply_add_fusion.3) | copy-start | bytes 772
  273.8 13.3 %copy-start.20 = (f32[1,24]{1,0:T(1,128)S(1)}, f32[1,24]{1,0:T(1,128)}, u32[]{:S(2)}) copy-start(f32[1,24]{1,0:T(1,128)} %param.10) | copy-start | bytes 292
  274.9 14.6 %copy-start.4 = (f32[1792]{0:T(1024)S(1)}, f32[1792]{0:T(1024)}, u32[]{:S(2)}) copy-start(f32[1792]{0:T(1024)} %copy-done.2) | copy-start | bytes 21508
  290.6 17.1 %all-to-all-start.4 = ((bf16[4,32,1792]{2,1,0:T(8,128)(2,1)}), bf16[4,32,1792]{2,1,0:T(8,128)(2,1)S(1)}, u32[]{:S(2)}, u32[]{:S(2)}) async-start(bf16[4,32,1792]{2,1,0:T(8,128)(2,1)} %bitcast.126), calls=%async_computation.4 | async-start | bytes 917504 | tf_op jit(solution)/shard_map/all_to_all | solution.py:89
  294.0 50.1 %all-reduce.11.cloned.1.call-start = ((), (), s32[]{:S(2)}) async-start(), calls=%async_computation.8 | async-start | bytes 1048576 | tf_op jit(solution)/shard_map/psum | solution.py:30
  346.4 16.7 %all-to-all-start.5 = ((bf16[4,32,1792]{2,1,0:T(8,128)(2,1)}), bf16[4,32,1792]{2,1,0:T(8,128)(2,1)S(1)}, u32[]{:S(2)}, u32[]{:S(2)}) async-start(bf16[4,32,1792]{2,1,0:T(8,128)(2,1)} %bitcast.138), calls=%async_computation.5 | async-start | bytes 917504 | tf_op jit(solution)/shard_map/all_to_all | solution.py:34
  351.0 12.3 %copy-start.21 = (f32[64]{0:T(128)S(1)}, f32[64]{0:T(128)}, u32[]{:S(2)}) copy-start(f32[64]{0:T(128)} %get-tuple-element.26) | copy-start | bytes 772
  351.0 12.3 %copy-start.25 = (s32[64]{0:T(128)S(1)}, s32[64]{0:T(128)}, u32[]{:S(2)}) copy-start(s32[64]{0:T(128)} %copy-done.24) | copy-start | bytes 772
  363.8 2.1 copy-start.30
  363.8 2.1 copy-start.31
  363.9 2.1 copy-start.32
Sparse Core Ops, SparseCore 0:
  68.2 33.9 all-reduce.6
  189.4 36.0 all-reduce.8
  311.3 32.8 all-reduce.10
where the time goes:
time: 380 us; the launch traced here: 376 us
  waiting for transfers between devices  166 us (44%)
  other arithmetic  63.2 us (17%)
  blocking collectives  38.8 us (10%)
  matrix products  35.5 us (9%)
  starting transfers between devices  34.3 us (9%)
  local copies, waits for them, and re-layouts  23.9 us (6%)
  between operations  13.8 us (4%)
    psum x3, waiting for transfers between devices, expert_block(): summed = lax.psum(hidden_pre, 'dp')  97.7 us
    psum x3, blocking collectives, mix_layer(): lax.psum((square_part, projected, path_gram), 'dp')  38.8 us
    ppermute x2, waiting for transfers between devices, passed_along(): lax.ppermute(value, axis, [(source, source + steps) for source in range(l...  33.3 us
    div x57, other arithmetic, doubly_stochastic_project(): stream_mixer = stream_mixer / jnp.sum(stream_mixer, axis=2, keepdims=True)  33 us
    all_to_all x3, waiting for transfers between devices, expert_block(): lax.all_to_all(expert_output_rows, 'expert', split_axis=0, concat_axis=0,...  22.4 us
    all_to_all x3, starting transfers between devices, expert_block(): lax.all_to_all(expert_output_rows, 'expert', split_axis=0, concat_axis=0,...  13.8 us
    all_to_all x3, waiting for transfers between devices, mix_layer(): lax.all_to_all(outgoing, 'expert', split_axis=0, concat_axis=0, tiled=True)  13 us
    all_to_all x3, starting transfers between devices, mix_layer(): lax.all_to_all(outgoing, 'expert', split_axis=0, concat_axis=0, tiled=True)  11.8 us
  transfers between devices with their start and end apart: 11, of which 9 were waited for; matrix products, arithmetic and copies ran while one was open for 15% of the time, Pallas kernels for 0%

commit v1 on v0

--- a/solution.py
+++ b/solution.py
@@ -27,7 +27,7 @@
     slot_rows = received.reshape(sources * items, width)
     inner = down_proj.shape[0]
     hidden_pre = jnp.dot(slot_rows, gate_up, preferred_element_type=jnp.float32)
-    summed = lax.psum(hidden_pre, "dp")
+    summed = jnp.sum(lax.all_gather(hidden_pre, "dp"), axis=0)
     hidden = (jax.nn.silu(summed[:, :inner]) * summed[:, inner:]).astype(jnp.bfloat16)
     expert_output_rows = jnp.dot(hidden, down_proj, preferred_element_type=jnp.float32)
     expert_output_rows = expert_output_rows.astype(jnp.bfloat16).reshape(sources, items, width)

time: 380 us -> 326 us (0.86)
  other arithmetic: 63.2 us -> 21.6 us
  local copies, waits for them, and re-layouts: 23.9 us -> 10.2 us
  waiting for transfers between devices: 166 us -> 173 us
    psum x3 -> x0, waiting for transfers between devices: 97.7 us -> none  [expert_block(): summed = lax.psum(hidden_pre, 'dp')]
    all_gather x0 -> x3, waiting for transfers between devices: none -> 66.5 us  [expert_block(): summed = jnp.sum(lax.all_gather(hidden_pre, 'dp'), axis=0)]
    div x57, other arithmetic: 33 us -> 2.1 us  [doubly_stochastic_project(): stream_mixer = stream_mixer / jnp.sum(stream_mixer, axis=2, keepdims=True)]
    all_to_all x3, waiting for transfers between devices: 13 us -> 31.5 us  [mix_layer(): lax.all_to_all(outgoing, 'expert', split_axis=0, concat_axis=0, tiled=True)]
    all_to_all x3, waiting for transfers between devices: 22.4 us -> 39.3 us  [expert_block(): lax.all_to_all(expert_output_rows, 'expert', split_axis=0, concat_axis=0,...]
    reduce_sum x0 -> x3, other arithmetic: none -> 5.41 us  [expert_block(): summed = jnp.sum(lax.all_gather(hidden_pre, 'dp'), axis=0)]
    unnamed x71 -> x21, local copies, waits for them, and re-layouts: 7.82 us -> 4.99 us
  transfers between devices with their start and end apart: 11 -> 11, of which waited for: 9 -> 11; matrix products, arithmetic and copies ran while one was open for 15% -> 3% of each run, Pallas kernels for 0% -> 0%
where the time goes in v1:
time: 326 us; the launch traced here: 325 us
  waiting for transfers between devices  173 us (53%)
  blocking collectives  39.8 us (12%)
  starting transfers between devices  34.3 us (11%)
  matrix products  31.8 us (10%)
  other arithmetic  21.6 us (7%)
  between operations  13.7 us (4%)
  local copies, waits for them, and re-layouts  10.2 us (3%)
    all_gather x3, waiting for transfers between devices, expert_block(): summed = jnp.sum(lax.all_gather(hidden_pre, 'dp'), axis=0)  66.5 us
    psum x3, blocking collectives, mix_layer(): lax.psum((square_part, projected, path_gram), 'dp')  39.8 us
    all_to_all x3, waiting for transfers between devices, expert_block(): lax.all_to_all(expert_output_rows, 'expert', split_axis=0, concat_axis=0,...  39.3 us
    ppermute x2, waiting for transfers between devices, passed_along(): lax.ppermute(value, axis, [(source, source + steps) for source in range(l...  35.8 us
    all_to_all x3, waiting for transfers between devices, mix_layer(): lax.all_to_all(outgoing, 'expert', split_axis=0, concat_axis=0, tiled=True)  31.5 us
    all_to_all x3, starting transfers between devices, expert_block(): lax.all_to_all(expert_output_rows, 'expert', split_axis=0, concat_axis=0,...  13.8 us
    all_to_all x3, starting transfers between devices, mix_layer(): lax.all_to_all(outgoing, 'expert', split_axis=0, concat_axis=0, tiled=True)  11.8 us
    dot_general x3, matrix products, expert_block(): hidden_pre = jnp.dot(slot_rows, gate_up, preferred_element_type=jnp.float32)  10.4 us
  transfers between devices with their start and end apart: 11, of which 11 were waited for; matrix products, arithmetic and copies ran while one was open for 3% of the time, Pallas kernels for 0%

profile of v1, /device:TPU:0, one launch (start us, length us, event | category | flops | bytes accessed | tf_op | source)
XLA Modules:
  0.0 324.7 jit_solution(3930974689896701733)
XLA Ops:
  6.5 1.6 constant_dynamic-slice_fusion.6
  8.2 0.4 fusion.60
  8.6 1.2 fusion.129
  9.8 0.4 convolution_bitcast_fusion.2
  10.1 15.1 %all-reduce.2 = (f32[64,24]{0,1:T(8,128)S(1)}, f32[64]{0:T(128)S(1)}, f32[64,4,4]{2,1,0:T(4,128)}) all-reduce(f32[64,24]{0,1:T(8,128)S(1)} %convolution_bitcast_fusion.2, f32[64]{0:T(128)S(1)} %get-tuple-element.18, f32[64,4,4]{2,1,0:T(4,128)S(1)} %fusion.129), channel_id=1, replica_groups=mesh['dp'=4,'section'=2,'expert'=4] {'dp'}, use_global_device_ids=true, to_apply=%region_0.1 | all-reduce | flops 2624 | bytes 20992 | tf_op jit(solution)/shard_map/psum | solution.py:43
  25.5 0.3 fusion.61
  25.8 1.5 fusion.265
  27.6 0.2 select_reduce_fusion.2
  27.9 0.3 convolution_convert_fusion.5
  28.2 0.8 broadcast_in_dim.81
  29.0 4.9 %all-to-all-start = ((bf16[4,32,1792]{2,1,0:T(8,128)(2,1)}), bf16[4,32,1792]{2,1,0:T(8,128)(2,1)S(1)}, u32[]{:S(2)}, u32[]{:S(2)}) async-start(bf16[4,32,1792]{2,1,0:T(8,128)(2,1)} %bitcast.131), calls=%async_computation | async-start | bytes 917504 | tf_op jit(solution)/shard_map/all_to_all | solution.py:89
  33.9 4.8 %copy.306 = bf16[224,8,2,512]{3,1,2,0:T(8,128)(2,1)} copy(bf16[224,8,2,512]{3,2,1,0:T(2,128)(2,1)} %bitcast.124) | data formatting | bytes 7340032
  38.8 7.1 %all-to-all-done = bf16[4,32,1792]{2,1,0:T(8,128)(2,1)S(1)} async-done(((bf16[4,32,1792]{2,1,0:T(8,128)(2,1)}), bf16[4,32,1792]{2,1,0:T(8,128)(2,1)S(1)}, u32[]{:S(2)}, u32[]{:S(2)}) %all-to-all-start) | async-done | bytes 458784 | tf_op jit(solution)/shard_map/all_to_all | solution.py:89
  45.9 3.5 %fusion.266 = f32[128,1024]{1,0:T(8,128)} fusion(bf16[128,1792]{1,0:T(8,128)(2,1)S(1)} %bitcast.128, bf16[1792,1024]{1,0:T(8,128)(2,1)} %bitcast.121), kind=kOutput, calls=%fused_computation.463 | convolution fusion | flops 469762048 | bytes 4653056 | tf_op jit(solution)/shard_map/dot_general | solution.py:29
  49.9 21.7 %all-gather.7.cloned.1.call-done = f32[512,1024]{1,0:T(8,128)} async-done(((f32[128,1024]{1,0:T(8,128)}), f32[512,1024]{1,0:T(8,128)}) %all-gather.7.cloned.1.call-update) | async-done | bytes 2097168 | tf_op jit(solution)/shard_map/all_gather | solution.py:30
  71.6 1.8 reduce_sum.1255
  73.5 1.2 convolution_convert_fusion.2
  74.7 4.6 %all-to-all-start.1 = ((bf16[4,32,1792]{2,1,0:T(8,128)(2,1)}), bf16[4,32,1792]{2,1,0:T(8,128)(2,1)S(1)}, u32[]{:S(2)}, u32[]{:S(2)}) async-start(bf16[4,32,1792]{2,1,0:T(8,128)(2,1)} %bitcast.145), calls=%async_computation.1 | async-start | bytes 917504 | tf_op jit(solution)/shard_map/all_to_all | solution.py:34
  79.6 13.1 %all-to-all-done.1 = bf16[4,32,1792]{2,1,0:T(8,128)(2,1)S(1)} async-done(((bf16[4,32,1792]{2,1,0:T(8,128)(2,1)}), bf16[4,32,1792]{2,1,0:T(8,128)(2,1)S(1)}, u32[]{:S(2)}, u32[]{:S(2)}) %all-to-all-start.1) | async-done | bytes 458784 | tf_op jit(solution)/shard_map/all_to_all | solution.py:34
  92.9 0.6 fusion.154
  93.5 3.2 fusion.57
  96.6 4.3 %collective-permute-start = (bf16[64,4,1792]{2,1,0:T(4,128)(2,1)}, bf16[64,4,1792]{2,1,0:T(4,128)(2,1)}, u32[]{:S(2)}, u32[]{:S(2)}) collective-permute-start(bf16[64,4,1792]{2,1,0:T(4,128)(2,1)} %fusion.57), channel_id=1, source_target_pairs={{0,4},{1,5},{2,6},{3,7},{8,12},{9,13},{10,14},{11,15},{16,20},{17,... | collective-permute-start | bytes 2752520 | tf_op jit(solution)/shard_map/ppermute | solution.py:15
  101.1 0.2 select_reduce_fusion.1
  101.3 17.9 %collective-permute-done = bf16[64,4,1792]{2,1,0:T(4,128)(2,1)} collective-permute-done((bf16[64,4,1792]{2,1,0:T(4,128)(2,1)}, bf16[64,4,1792]{2,1,0:T(4,128)(2,1)}, u32[]{:S(2)}, u32[]{:S(2)}) %collective-permute-start) | collective-permute-done | bytes 917536 | tf_op jit(solution)/shard_map/ppermute | solution.py:15
  119.2 2.6 fusion.62
  121.8 1.1 fusion.267
  122.9 0.4 convolution_bitcast_fusion.1
  123.3 12.3 %all-reduce.1 = (f32[64,24]{0,1:T(8,128)S(1)}, f32[64]{0:T(128)S(1)}, f32[64,4,4]{2,1,0:T(4,128)S(1)}) all-reduce(f32[64,24]{0,1:T(8,128)S(1)} %convolution_bitcast_fusion.1, f32[64]{0:T(128)S(1)} %get-tuple-element.16, f32[64,4,4]{2,1,0:T(4,128)S(1)} %fusion.267), channel_id=1, replica_groups=mesh['dp'=4,'section'=2,'expert'=4] {'dp'}, use_global_device_ids=true, to_apply=%region_48.49 | all-reduce | flops 2624 | bytes 20992 | tf_op jit(solution)/shard_map/psum | solution.py:43
  135.9 1.3 fusion.63
  137.2 0.6 fusion.268
  137.9 0.3 convolution_convert_fusion.4
  138.2 0.8 broadcast_in_dim.84
  139.0 3.5 %all-to-all-start.2 = ((bf16[4,32,1792]{2,1,0:T(8,128)(2,1)}), bf16[4,32,1792]{2,1,0:T(8,128)(2,1)S(1)}, u32[]{:S(2)}, u32[]{:S(2)}) async-start(bf16[4,32,1792]{2,1,0:T(8,128)(2,1)} %bitcast.132), calls=%async_computation.2 | async-start | bytes 917504 | tf_op jit(solution)/shard_map/all_to_all | solution.py:89
  142.6 12.2 %all-to-all-done.2 = bf16[4,32,1792]{2,1,0:T(8,128)(2,1)S(1)} async-done(((bf16[4,32,1792]{2,1,0:T(8,128)(2,1)}), bf16[4,32,1792]{2,1,0:T(8,128)(2,1)S(1)}, u32[]{:S(2)}, u32[]{:S(2)}) %all-to-all-start.2) | async-done | bytes 458784 | tf_op jit(solution)/shard_map/all_to_all | solution.py:89
  154.9 3.5 %fusion.269 = f32[128,1024]{1,0:T(8,128)} fusion(bf16[128,1792]{1,0:T(8,128)(2,1)S(1)} %bitcast.130, bf16[1792,1024]{1,0:T(8,128)(2,1)} %bitcast.122), kind=kOutput, calls=%fused_computation.466 | convolution fusion | flops 469762048 | bytes 4653056 | tf_op jit(solution)/shard_map/dot_general | solution.py:29
  158.9 22.4 %all-gather.9.cloned.1.call-done = f32[512,1024]{1,0:T(8,128)} async-done(((f32[128,1024]{1,0:T(8,128)}), f32[512,1024]{1,0:T(8,128)}) %all-gather.9.cloned.1.call-update) | async-done | bytes 2097168 | tf_op jit(solution)/shard_map/all_gather | solution.py:30
  181.3 1.8 reduce_sum.1299
  183.1 1.2 convolution_convert_fusion.1
  184.3 4.6 %all-to-all-start.3 = ((bf16[4,32,1792]{2,1,0:T(8,128)(2,1)}), bf16[4,32,1792]{2,1,0:T(8,128)(2,1)S(1)}, u32[]{:S(2)}, u32[]{:S(2)}) async-start(bf16[4,32,1792]{2,1,0:T(8,128)(2,1)} %bitcast.143), calls=%async_computation.3 | async-start | bytes 917504 | tf_op jit(solution)/shard_map/all_to_all | solution.py:34
  189.3 13.1 %all-to-all-done.3 = bf16[4,32,1792]{2,1,0:T(8,128)(2,1)S(1)} async-done(((bf16[4,32,1792]{2,1,0:T(8,128)(2,1)}), bf16[4,32,1792]{2,1,0:T(8,128)(2,1)S(1)}, u32[]{:S(2)}, u32[]{:S(2)}) %all-to-all-start.3) | async-done | bytes 458784 | tf_op jit(solution)/shard_map/all_to_all | solution.py:34
  202.6 0.6 fusion.152
  203.1 3.0 fusion.58
  206.1 4.3 %collective-permute-start.1 = (bf16[64,4,1792]{2,1,0:T(4,128)(2,1)}, bf16[64,4,1792]{2,1,0:T(4,128)(2,1)}, u32[]{:S(2)}, u32[]{:S(2)}) collective-permute-start(bf16[64,4,1792]{2,1,0:T(4,128)(2,1)} %fusion.58), channel_id=1, source_target_pairs={{0,4},{1,5},{2,6},{3,7},{8,12},{9,13},{10,14},{11,15},{16,20},{17,... | collective-permute-start | bytes 2752520 | tf_op jit(solution)/shard_map/ppermute | solution.py:15
  210.5 0.2 select_reduce_fusion
  210.7 17.9 %collective-permute-done.1 = bf16[64,4,1792]{2,1,0:T(4,128)(2,1)} collective-permute-done((bf16[64,4,1792]{2,1,0:T(4,128)(2,1)}, bf16[64,4,1792]{2,1,0:T(4,128)(2,1)}, u32[]{:S(2)}, u32[]{:S(2)}) %collective-permute-start.1) | collective-permute-done | bytes 917536 | tf_op jit(solution)/shard_map/ppermute | solution.py:15
  228.7 2.6 fusion.64
  231.3 1.1 fusion.270
  232.4 0.4 convolution_bitcast_fusion
  232.7 12.4 %all-reduce = (f32[64,24]{0,1:T(8,128)S(1)}, f32[64]{0:T(128)S(1)}, f32[64,4,4]{2,1,0:T(4,128)S(1)}) all-reduce(f32[64,24]{0,1:T(8,128)S(1)} %convolution_bitcast_fusion, f32[64]{0:T(128)S(1)} %get-tuple-element.14, f32[64,4,4]{2,1,0:T(4,128)S(1)} %fusion.270), channel_id=1, replica_groups=mesh['dp'=4,'section'=2,'expert'=4] {'dp'}, use_global_device_ids=true, to_apply=%region_96.97 | all-reduce | flops 2624 | bytes 20992 | tf_op jit(solution)/shard_map/psum | solution.py:43
  245.4 1.3 fusion.65
  246.7 0.6 fusion.271
  247.4 0.3 convolution_convert_fusion.3
  247.7 0.8 broadcast_in_dim.87
  248.5 3.5 %all-to-all-start.4 = ((bf16[4,32,1792]{2,1,0:T(8,128)(2,1)}), bf16[4,32,1792]{2,1,0:T(8,128)(2,1)S(1)}, u32[]{:S(2)}, u32[]{:S(2)}) async-start(bf16[4,32,1792]{2,1,0:T(8,128)(2,1)} %bitcast.133), calls=%async_computation.4 | async-start | bytes 917504 | tf_op jit(solution)/shard_map/all_to_all | solution.py:89
  252.2 12.2 %all-to-all-done.4 = bf16[4,32,1792]{2,1,0:T(8,128)(2,1)S(1)} async-done(((bf16[4,32,1792]{2,1,0:T(8,128)(2,1)}), bf16[4,32,1792]{2,1,0:T(8,128)(2,1)S(1)}, u32[]{:S(2)}, u32[]{:S(2)}) %all-to-all-start.4) | async-done | bytes 458784 | tf_op jit(solution)/shard_map/all_to_all | solution.py:89
  264.4 3.5 %fusion.272 = f32[128,1024]{1,0:T(8,128)} fusion(bf16[128,1792]{1,0:T(8,128)(2,1)S(1)} %bitcast.129, bf16[1792,1024]{1,0:T(8,128)(2,1)} %bitcast.123), kind=kOutput, calls=%fused_computation.469 | convolution fusion | flops 469762048 | bytes 4653056 | tf_op jit(solution)/shard_map/dot_general | solution.py:29
  268.5 22.4 %all-gather.11.cloned.1.call-done = f32[512,1024]{1,0:T(8,128)} async-done(((f32[128,1024]{1,0:T(8,128)}), f32[512,1024]{1,0:T(8,128)}) %all-gather.11.cloned.1.call-update) | async-done | bytes 2097168 | tf_op jit(solution)/shard_map/all_gather | solution.py:30
  290.8 1.8 reduce_sum.1343
  292.6 1.2 convolution_convert_fusion
  293.9 4.6 %all-to-all-start.5 = ((bf16[4,32,1792]{2,1,0:T(8,128)(2,1)}), bf16[4,32,1792]{2,1,0:T(8,128)(2,1)S(1)}, u32[]{:S(2)}, u32[]{:S(2)}) async-start(bf16[4,32,1792]{2,1,0:T(8,128)(2,1)} %bitcast.144), calls=%async_computation.5 | async-start | bytes 917504 | tf_op jit(solution)/shard_map/all_to_all | solution.py:34
  298.8 13.1 %all-to-all-done.5 = bf16[4,32,1792]{2,1,0:T(8,128)(2,1)S(1)} async-done(((bf16[4,32,1792]{2,1,0:T(8,128)(2,1)}), bf16[4,32,1792]{2,1,0:T(8,128)(2,1)S(1)}, u32[]{:S(2)}, u32[]{:S(2)}) %all-to-all-start.5) | async-done | bytes 458784 | tf_op jit(solution)/shard_map/all_to_all | solution.py:34
  312.1 0.6 fusion.150
  312.6 2.0 fusion.59
  314.7 3.4 %select_select_fusion = bf16[1,2,64,4,1792]{4,3,2,1,0:T(4,128)(2,1)} fusion(pred[2]{0:T(512)(128)(4,1)S(1)} %iota_compare_fusion.13, pred[2]{0:T(512)(128)(4,1)S(1)} %iota_compare_fusion.14, pred[2]{0:T(512)(128)(4,1)S(1)} %iota_compare_fusion.12, bf16[64,4,1792]{2,1,0:T(4,128)(2,1)} %fusion.57, bf16[64,4,1792]{2,1,0:T(4,128)(2,1)} %fusion.58, ...), kind=kLoop, calls=%fused_computation.84 | loop fusion | flops 2752512 | bytes 4587526 | tf_op jit(solution)/shard_map/jit(_where)/select_n | solution.py:131
  (141 shorter events, 5.2 us)
Async XLA Ops:
  6.5 66.9 %copy-start = (bf16[1,1,512,1792]{3,2,1,0:T(8,128)(2,1)S(1)}, bf16[1,1,512,1792]{3,2,1,0:T(8,128)(2,1)}, u32[]{:S(2)}) copy-start(bf16[1,1,512,1792]{3,2,1,0:T(8,128)(2,1)} %param.13) | copy-start | bytes 5505028
  8.5 1.2 copy-start.1
  8.5 16.7 %copy-start.5 = (f32[1,24]{1,0:T(1,128)S(1)}, f32[1,24]{1,0:T(1,128)}, u32[]{:S(2)}) copy-start(f32[1,24]{1,0:T(1,128)} %param.10) | copy-start | bytes 292
  9.8 17.7 %copy-start.6 = (s32[1,2,64,1]{2,3,1,0:T(1,128)S(1)}, s32[1,2,64,1]{2,3,1,0:T(1,128)}, u32[]{:S(2)}) copy-start(s32[1,2,64,1]{2,3,1,0:T(1,128)} %param.14) | copy-start | bytes 1540
  9.8 18.1 %copy-start.4 = (bf16[1,1792]{1,0:T(2,128)(2,1)S(1)}, bf16[1,1792]{1,0:T(2,128)(2,1)}, u32[]{:S(2)}) copy-start(bf16[1,1792]{1,0:T(2,128)(2,1)} %param.11) | copy-start | bytes 10756
  29.0 16.9 %all-to-all-start = ((bf16[4,32,1792]{2,1,0:T(8,128)(2,1)}), bf16[4,32,1792]{2,1,0:T(8,128)(2,1)S(1)}, u32[]{:S(2)}, u32[]{:S(2)}) async-start(bf16[4,32,1792]{2,1,0:T(8,128)(2,1)} %bitcast.131), calls=%async_computation | async-start | bytes 917504 | tf_op jit(solution)/shard_map/all_to_all | solution.py:89
  33.8 37.8 %all-gather.7.cloned.1.call-start = ((), (), s32[]{:S(2)}) async-start(), calls=%async_computation.6 | async-start | bytes 2621440 | tf_op jit(solution)/shard_map/all_gather | solution.py:30
  73.5 6.1 %copy-start.7 = (f32[1,2,64,1]{2,3,1,0:T(1,128)S(1)}, f32[1,2,64,1]{2,3,1,0:T(1,128)}, u32[]{:S(2)}) copy-start(f32[1,2,64,1]{2,3,1,0:T(1,128)} %param.15) | copy-start | bytes 1540
  74.7 18.1 %all-to-all-start.1 = ((bf16[4,32,1792]{2,1,0:T(8,128)(2,1)}), bf16[4,32,1792]{2,1,0:T(8,128)(2,1)S(1)}, u32[]{:S(2)}, u32[]{:S(2)}) async-start(bf16[4,32,1792]{2,1,0:T(8,128)(2,1)} %bitcast.145), calls=%async_computation.1 | async-start | bytes 917504 | tf_op jit(solution)/shard_map/all_to_all | solution.py:34
  96.6 22.6 %collective-permute-start = (bf16[64,4,1792]{2,1,0:T(4,128)(2,1)}, bf16[64,4,1792]{2,1,0:T(4,128)(2,1)}, u32[]{:S(2)}, u32[]{:S(2)}) collective-permute-start(bf16[64,4,1792]{2,1,0:T(4,128)(2,1)} %fusion.57), channel_id=1, source_target_pairs={{0,4},{1,5},{2,6},{3,7},{8,12},{9,13},{10,14},{11,15},{16,20},{17,... | collective-permute-start | bytes 2752520 | tf_op jit(solution)/shard_map/ppermute | solution.py:15
  121.8 1.1 copy-start.2
  139.0 15.9 %all-to-all-start.2 = ((bf16[4,32,1792]{2,1,0:T(8,128)(2,1)}), bf16[4,32,1792]{2,1,0:T(8,128)(2,1)S(1)}, u32[]{:S(2)}, u32[]{:S(2)}) async-start(bf16[4,32,1792]{2,1,0:T(8,128)(2,1)} %bitcast.132), calls=%async_computation.2 | async-start | bytes 917504 | tf_op jit(solution)/shard_map/all_to_all | solution.py:89
  142.5 38.9 %all-gather.9.cloned.1.call-start = ((), (), s32[]{:S(2)}) async-start(), calls=%async_computation.7 | async-start | bytes 2621440 | tf_op jit(solution)/shard_map/all_gather | solution.py:30
  184.3 18.1 %all-to-all-start.3 = ((bf16[4,32,1792]{2,1,0:T(8,128)(2,1)}), bf16[4,32,1792]{2,1,0:T(8,128)(2,1)S(1)}, u32[]{:S(2)}, u32[]{:S(2)}) async-start(bf16[4,32,1792]{2,1,0:T(8,128)(2,1)} %bitcast.143), calls=%async_computation.3 | async-start | bytes 917504 | tf_op jit(solution)/shard_map/all_to_all | solution.py:34
  206.1 22.6 %collective-permute-start.1 = (bf16[64,4,1792]{2,1,0:T(4,128)(2,1)}, bf16[64,4,1792]{2,1,0:T(4,128)(2,1)}, u32[]{:S(2)}, u32[]{:S(2)}) collective-permute-start(bf16[64,4,1792]{2,1,0:T(4,128)(2,1)} %fusion.58), channel_id=1, source_target_pairs={{0,4},{1,5},{2,6},{3,7},{8,12},{9,13},{10,14},{11,15},{16,20},{17,... | collective-permute-start | bytes 2752520 | tf_op jit(solution)/shard_map/ppermute | solution.py:15
  231.3 1.1 copy-start.3
  248.5 15.9 %all-to-all-start.4 = ((bf16[4,32,1792]{2,1,0:T(8,128)(2,1)}), bf16[4,32,1792]{2,1,0:T(8,128)(2,1)S(1)}, u32[]{:S(2)}, u32[]{:S(2)}) async-start(bf16[4,32,1792]{2,1,0:T(8,128)(2,1)} %bitcast.133), calls=%async_computation.4 | async-start | bytes 917504 | tf_op jit(solution)/shard_map/all_to_all | solution.py:89
  252.0 38.9 %all-gather.11.cloned.1.call-start = ((), (), s32[]{:S(2)}) async-start(), calls=%async_computation.8 | async-start | bytes 2621440 | tf_op jit(solution)/shard_map/all_gather | solution.py:30
  293.9 18.1 %all-to-all-start.5 = ((bf16[4,32,1792]{2,1,0:T(8,128)(2,1)}), bf16[4,32,1792]{2,1,0:T(8,128)(2,1)S(1)}, u32[]{:S(2)}, u32[]{:S(2)}) async-start(bf16[4,32,1792]{2,1,0:T(8,128)(2,1)} %bitcast.144), calls=%async_computation.5 | async-start | bytes 917504 | tf_op jit(solution)/shard_map/all_to_all | solution.py:34
Sparse Core Ops, SparseCore 0:
  49.5 22.0 all-gather.6
  158.5 22.7 all-gather.8
  268.0 22.7 all-gather.10
